TPU v7x, 32 devices: a 4x4x1 block of a 4x4x8 slice. The times are simulated.
32 devices in a mesh: dp: 1 (over z), tp: 4 (over y), sp: 8 (over x, core).
Axes of the slice: x: 4, y: 4, z: 1, core: 2. Of those that a mesh axis runs over, the one named last changes fastest.
The devices are a block of a 4x4x8 slice.
Arguments:
- hidden: bfloat16 [16, 4096], P('dp')
- k_cache: bfloat16 [16, 4096, 32, 128], P('dp', 'sp', 'tp')
- v_cache: bfloat16 [16, 4096, 32, 128], P('dp', 'sp', 'tp')
- lengths: int32 [16], P('dp')
- rel_table: bfloat16 [4096, 32, 128], P('sp', 'tp')
- u_bias: bfloat16 [32, 128], P('tp')
- w_bias: bfloat16 [32, 128], P('tp')
- g_attn: bfloat16 [4096], replicated
- w_query: bfloat16 [4096, 32, 128], P(None, 'tp')
- w_key: bfloat16 [4096, 32, 128], P(None, 'tp')
- w_value: bfloat16 [4096, 32, 128], P(None, 'tp')
- w_out: bfloat16 [32, 128, 4096], P('tp')
- g_mlp: bfloat16 [4096], replicated
- w_up: bfloat16 [4096, 16384], P(None, 'tp')
- w_down: bfloat16 [16384, 4096], P('tp')
Outputs:
- output: bfloat16 [16, 4096], P('dp')
All inputs are finite; a program needn't handle non-finite values.
Results may differ from a plain program's by a relative error of at most 0.014473.
Values sent between devices are 32-bit elements.
A program may use at most 768 MiB of HBM per device.

v0:
```python
import functools

import jax
import jax.numpy as jnp
from jax import lax
from jax.experimental import pallas as pl
from jax.experimental.pallas import tpu as pltpu
from jax.sharding import PartitionSpec as P

EPS = 1e-6
MASKED = -1e30
CORES = 2
CHUNKS = 4
UP_PARTS = 8
OUT_PARTS = 2
FLOOR = -5e29
LANES = 128
F32 = jnp.float32
BF16 = jnp.bfloat16
NT = (((1,), (1,)), ((), ()))


def layer_kernel(n_sp, n_tp,
                 lens_in, hid_in, u_in, w_in, ga_in, gm_in, rel_hbm, k_hbm, v_hbm, wq_hbm, wk_hbm, wv_hbm, wo_hbm, wu_hbm, wd_hbm,
                 out_ref,
                 lens, hid, u_ref, w_ref, ga, gm,
                 wqb, wkvb, normed, spread_x, relb, rrev, kb, vb, wob, wdb,
                 kvsend, kvrecv, qall, qcb, relsend, grid_rel0, grid_rel1, grid_rel2, grid_rel3, win, sc, csend, crecv, call, aosend, aorecv,
                 x1all, aall, dnsend, dnrecv, oall,
                 hsem, ssem, rsem, rel_ssem, rel_rsem, fwd_ssem, fwd_rsem, relay_ssem, sib_ssem, sib_rsem, ctx_ssem, ctx_rsem, a_ssem, a_rsem, tp_ssem, tp_rsem):
    me = lax.axis_index('sp')
    my_tp = lax.axis_index('tp')
    batch = hid.shape[0]
    heads = u_ref.shape[0]
    head_dim = u_ref.shape[1]
    rows = kb.shape[1]
    seq_blk = rows // heads
    kk = wkvb.shape[1] // heads
    pieces = 8
    chunks = CHUNKS
    chunk = batch // chunks
    chips = n_sp // CORES
    chip, core = me // CORES, me % CORES
    sibling = chip * CORES + 1 - core
    co = wob.shape[1]
    per_row = LANES // heads
    rel_rows = seq_blk // per_row
    smax = seq_blk * n_sp
    half = rows // 2
    half_ff = wu_hbm.shape[1] // CORES
    scale = head_dim ** -0.5

    grid_rel = (grid_rel0, grid_rel1, grid_rel2, grid_rel3)
    copies = []

    def fetch(src, dst, sem=None):
        copy = pltpu.make_async_copy(src, dst, hsem.at[len(copies) if sem is None else sem])
        if sem is None:
            copies.append(copy)
        copy.start()
        return copy

    small = [fetch(hid_in, hid), fetch(ga_in, ga), fetch(u_in, u_ref), fetch(w_in, w_ref), fetch(gm_in, gm), fetch(lens_in, lens)]
    rel_copy = fetch(rel_hbm, relb)
    first_q = len(copies)
    piece = wqb.shape[0] // pieces
    q_copies = [fetch(wq_hbm.at[i * piece:(i + 1) * piece], wqb.at[i * piece:(i + 1) * piece]) for i in range(pieces)]
    w_rows = pl.ds(pl.multiple_of(me * kk * heads, kk * heads), kk * heads)
    w_copies = [fetch(src.at[w_rows], wkvb.at[i]) for i, src in enumerate((wk_hbm, wv_hbm))]
    k_copies = [fetch(k_hbm.at[g * chunk:(g + 1) * chunk], kb.at[g * chunk:(g + 1) * chunk]) for g in range(chunks)]
    v_copies = [fetch(v_hbm.at[g * chunk:(g + 1) * chunk], vb.at[g * chunk:(g + 1) * chunk]) for g in range(chunks)]
    o_cols = pl.ds(pl.multiple_of(me * co, co), co)
    wo_copy = fetch(wo_hbm.at[:, o_cols], wob)
    wd_copy = fetch(wd_hbm.at[:, o_cols], wdb)

    peers = [(lax.rem(chip + dx, chips) * CORES + (core if e == 0 else 1 - core))
             for dx in sorted(range(chips), key=lambda d: -min(d, chips - d)) for e in range(CORES) if (dx, e) != (0, 0)]

    def tp_peer(off):
        return lax.rem(my_tp + off, n_tp)

    for part in grid_rel:
        part[...] = jnp.zeros_like(part)

    barrier = pltpu.get_barrier_semaphore()
    for peer in peers:
        pl.semaphore_signal(barrier, inc=1, device_id={'sp': peer}, device_id_type=pl.DeviceIdType.MESH)
    for off in range(1, n_tp):
        pl.semaphore_signal(barrier, inc=1, device_id={'tp': tp_peer(off)}, device_id_type=pl.DeviceIdType.MESH)

    def remote(src, dst, send, recv, where):
        return pltpu.make_async_remote_copy(src_ref=src, dst_ref=dst, send_sem=send, recv_sem=recv, device_id=where,
                                            device_id_type=pl.DeviceIdType.MESH)

    sends = []

    def later(src, sem):
        sends.append(lambda: remote(src, src, sem, sem, {'sp': sibling}).wait_send())

    def take(dst, sem):
        remote(dst, dst, sem, sem, {'sp': sibling}).wait_recv()

    others = slice(0, n_sp - 1)

    def scatter(phase, src, dst):
        for peer in peers:
            remote(src.at[peer], dst.at[me], ssem.at[phase], rsem.at[phase], {'sp': peer}).start()
        later(src.at[others], ssem.at[phase])

    def gather(phase, buf, part=None):
        block = buf.at[me] if part is None else buf.at[me, part]
        for peer in peers:
            remote(block, block, ssem.at[phase], rsem.at[phase], {'sp': peer}).start()
        if part is None or part == buf.shape[1] - 1:
            later(buf.at[others], ssem.at[phase])

    def arrived(phase, buf):
        take(buf.at[others], rsem.at[phase])

    def tp_send(phase, part, src, dst):
        dst[part, my_tp] = src[part]
        for off in sorted(range(1, n_tp), key=lambda d: -min(d, n_tp - d)):
            remote(src.at[part], dst.at[part, my_tp], tp_ssem.at[phase, part], tp_rsem.at[phase, part], {'tp': tp_peer(off)}).start()
        later(dst.at[part, 0:n_tp - 1], tp_ssem.at[phase, part])

    def tp_total(phase, part, dst):
        take(dst.at[part, 0:n_tp - 1], tp_rsem.at[phase, part])
        total = dst[part, 0]
        for t in range(1, n_tp):
            total = total + dst[part, t]
        return total

    for copy in small:
        copy.wait()
    wide = hid[...].astype(F32)
    inv = lax.rsqrt(jnp.mean(wide * wide, axis=-1, keepdims=True) + EPS)
    whole = (wide * inv * ga[...].reshape(1, wide.shape[1]).astype(F32)).astype(BF16)
    n_in = wide.shape[1] // LANES
    for c in range(n_in):
        normed[c * batch:(c + 1) * batch] = whole[:, c * LANES:(c + 1) * LANES]
    span = LANES * heads
    spread = (lax.broadcasted_iota(jnp.int32, (LANES, span), 1) // heads
              == lax.broadcasted_iota(jnp.int32, (LANES, span), 0)).astype(F32).astype(BF16)
    lane_head = lax.broadcasted_iota(jnp.int32, (batch, LANES), 1) % heads
    head_mask = [jnp.concatenate([(lane_head == h).astype(F32).astype(BF16)] * heads, axis=1) for h in range(heads)]

    spread_x[...] = jnp.dot(normed[...], spread, preferred_element_type=F32).astype(BF16)

    def by_head(c):
        spread_in = spread_x[pl.ds(pl.multiple_of(c * batch, batch), batch), :]
        return jnp.concatenate([spread_in * head_mask[h] for h in range(heads)], axis=0)

    rel_copy.wait()
    group = 32

    def reverse(i, carry):
        tile = relb[pl.ds(pl.multiple_of(i * group, group), group)].astype(F32)
        flipped = jnp.concatenate([tile[group - 1 - j:group - j] for j in range(group)], axis=0)
        flipped = flipped.reshape(group * heads, head_dim).astype(BF16)
        at = pl.multiple_of((seq_blk // group - 1 - i) * group * heads, group * heads)
        rrev[pl.ds(at, group * heads), :] = flipped
        return carry

    lax.fori_loop(0, seq_blk // group, reverse, 0)

    def project(i, acc):
        pltpu.make_async_copy(wq_hbm.at[pl.ds(0, piece)], wqb.at[pl.ds(0, piece)], hsem.at[first_q + i]).wait()
        per = piece // span
        for j in range(per):
            at = pl.multiple_of((i * per + j) * span, span)
            acc = acc + jnp.dot(by_head(i * per + j), wqb[pl.ds(at, span), :], preferred_element_type=F32)
        return acc

    acc = lax.fori_loop(0, pieces, project, jnp.zeros((heads * batch, head_dim), F32))
    for h in range(heads):
        qall[h] = acc[h * batch:(h + 1) * batch].astype(BF16).astype(F32)

    u_wide, w_wide = u_ref[...].astype(F32), w_ref[...].astype(F32)
    q_pos = jnp.concatenate([(qall[h] + w_wide[h:h + 1]).astype(BF16) for h in range(heads)], axis=0)

    def relative(c, carry):
        tiles_now = 4
        wide_span = tiles_now * LANES
        table = rrev[c * wide_span:(c + 1) * wide_span, :]
        scores = lax.dot_general(q_pos, table, NT, preferred_element_type=F32)
        for t in range(tiles_now):
            tile = scores[:, t * LANES:(t + 1) * LANES]
            row = tile[:batch]
            for h in range(1, heads):
                row = jnp.where(lane_head == h, tile[h * batch:(h + 1) * batch], row)
            at = tiles_now * c + t
            relsend[:, at:at + 1, :] = row.reshape(batch, 1, LANES)
        return carry

    for c in range(rows // (4 * LANES)):
        relative(c, 0)

    half_rows = rel_rows // CORES

    def seqs(g):
        return pl.ds(g * chunk, chunk)

    def spot(src, to_chip, g, first, size):
        at = (n_sp - 1 - src - CORES * to_chip) * rel_rows + first
        return grid_rel[g].at[:, pl.ds(pl.multiple_of(at, half_rows), size), :]

    def needed(a, b):
        return a + b <= chips - 1

    def rel_out(g, act):
        for dx in range(1, chips):
            to_chip = lax.rem(chip + dx, chips)

            @pl.when(needed(to_chip, chip))
            def _():
                for part in range(CORES):
                    if 2 * dx == chips and part == 1:
                        continue
                    act(remote(relsend.at[seqs(g), part * half_rows:(part + 1) * half_rows, :],
                               spot(me, to_chip, g, part * half_rows, half_rows),
                               rel_ssem.at[dx], rel_rsem.at[chip, g], {'sp': to_chip * CORES + part}))

        @pl.when(needed(chip, chip))
        def _():
            act(remote(relsend.at[seqs(g)], spot(me, chip, g, 0, rel_rows), sib_ssem.at[0], sib_rsem.at[g], {'sp': sibling}))

    def each_source(fn):
        for dx in range(1, chips):
            from_chip = lax.rem(chip + dx, chips)

            @pl.when(needed(from_chip, chip))
            def _():
                fn(dx, from_chip)

    def pass_on(g, dx, from_chip, c, act):
        src = from_chip * CORES + c
        mine = spot(src, chip, g, core * half_rows, half_rows)
        act(remote(mine, mine, fwd_ssem.at[dx], fwd_rsem.at[from_chip, g], {'sp': sibling}))
        if dx == 1:
            to_chip = lax.rem(chip + chips - 1, chips)

            @pl.when(jnp.logical_and(core == 1, needed(to_chip, from_chip)))
            def _():
                act(remote(mine, spot(src, to_chip, g, half_rows, half_rows), relay_ssem.at[0], rel_rsem.at[from_chip, g],
                           {'sp': to_chip * CORES + 1}))

    both = relsend.at[0:chunk]

    def rel_in(g):
        def fn(dx, from_chip):
            take(both, rel_rsem.at[from_chip, g])
            for c in range(CORES):
                pass_on(g, dx, from_chip, c, lambda copy: copy.start())

        each_source(fn)

    def rel_done(g):
        each_source(lambda dx, from_chip: take(both, fwd_rsem.at[from_chip, g]))

        @pl.when(needed(chip, chip))
        def _():
            take(both, sib_rsem.at[g])

    def rel_sent():
        for dx in range(1, chips):
            to_chip = lax.rem(chip + dx, chips)
            sent = relsend.at[:, 0:half_rows] if 2 * dx == chips else relsend

            @pl.when(needed(to_chip, chip))
            def _():
                remote(sent, sent, rel_ssem.at[dx], rel_ssem.at[dx], {'sp': sibling}).wait_send()
                remote(relsend, relsend, fwd_ssem.at[dx], fwd_ssem.at[dx], {'sp': sibling}).wait_send()

        @pl.when(needed(chip, chip))
        def _():
            remote(relsend, relsend, sib_ssem.at[0], sib_ssem.at[0], {'sp': sibling}).wait_send()

        to_chip, from_chip = lax.rem(chip + chips - 1, chips), lax.rem(chip + 1, chips)

        @pl.when(jnp.logical_and(jnp.logical_and(core == 1, needed(from_chip, chip)), needed(to_chip, from_chip)))
        def _():
            remote(relsend, relsend, relay_ssem.at[0], relay_ssem.at[0], {'sp': sibling}).wait_send()

    pl.semaphore_wait(barrier, n_sp + n_tp - 2)
    rel_out(0, lambda copy: copy.start())

    @pl.when(needed(chip, chip))
    def _():
        at = pl.multiple_of((n_sp - 1 - me - CORES * chip) * rel_rows, rel_rows)
        for g in range(chunks):
            grid_rel[g][:, pl.ds(at, rel_rows), :] = relsend[seqs(g)]

    for i in range(2):
        w_copies[i].wait()
    lhs_first = me * (kk // LANES)
    acc = [jnp.zeros((heads * batch, head_dim), F32)] * 2
    for c in range(kk // LANES):
        lhs = by_head(lhs_first + c)
        acc = [acc[i] + jnp.dot(lhs, wkvb[i, c * span:(c + 1) * span, :], preferred_element_type=F32) for i in range(2)]
    for i in range(2):
        for h in range(heads):
            kvsend[h, i] = acc[i][h * batch:(h + 1) * batch]
    scatter(0, kvsend, kvrecv)
    kvrecv[me] = kvsend[me]

    rel_out(1, lambda copy: copy.start())
    for h in range(heads):
        qcb[:, h:h + 1, :] = (qall[h] + u_wide[h:h + 1]).reshape(batch, 1, head_dim)

    def content_of(g):
        k_copies[g].wait()
        for j in range(chunk):
            b = g * chunk + j
            q = qcb[b]
            zero = jnp.zeros_like(q)
            two = jnp.concatenate([jnp.concatenate([q, zero], axis=1), jnp.concatenate([zero, q], axis=1)], axis=0).astype(BF16)
            for c in range(half // 256):
                keys = jnp.concatenate([kb[b, c * 256:(c + 1) * 256, :], kb[b, half + c * 256:half + (c + 1) * 256, :]], axis=1)
                sc[b, :, c * 256:(c + 1) * 256] = lax.dot_general(two, keys, NT, preferred_element_type=F32)

    r_iota = lax.broadcasted_iota(jnp.int32, (2 * heads, LANES), 0)
    l_iota = lax.broadcasted_iota(jnp.int32, (2 * heads, LANES), 1)
    slot = me * seq_blk + (r_iota // heads) * (seq_blk // 2) + l_iota // heads
    slot = jnp.where(r_iota % heads == l_iota % heads, slot, jnp.int32(2 ** 30))
    lane_row = lax.broadcasted_iota(jnp.int32, (rel_rows, LANES), 1)
    first_stat = lax.broadcasted_iota(jnp.int32, (heads, LANES), 1) < LANES // 2
    tiles = half // LANES

    def attend(g, j):
        b = g * chunk + j
        n = lens[b]
        start = smax - 1 - n
        row0 = jnp.minimum(start // per_row + core * rel_rows, n_sp * rel_rows - 1)
        turn = LANES - heads * (start % per_row)
        now = pltpu.roll(grid_rel[g][j, pl.ds(row0, rel_rows), :], turn, 1)
        after = pltpu.roll(grid_rel[g][j, pl.ds(row0 + 1, rel_rows), :], turn, 1)
        win[b] = jnp.where(lane_row < turn, now, after)
        scores = []
        for c in range(tiles):
            rel = jnp.concatenate([jnp.broadcast_to(win[b, c:c + 1, :], (heads, LANES)),
                                   jnp.broadcast_to(win[b, tiles + c:tiles + c + 1, :], (heads, LANES))], axis=0)
            s = (sc[b, :, c * LANES:(c + 1) * LANES] + rel) * scale
            scores.append(jnp.where(slot < n - c * per_row, s, MASKED))
        top = functools.reduce(jnp.maximum, scores)
        top = jnp.max(top, axis=1, keepdims=True)
        top = jnp.maximum(jnp.maximum(top[:heads], top[heads:]), FLOOR)
        top2 = jnp.concatenate([top, top], axis=0)
        weights = [jnp.exp(s - top2) for s in scores]
        total = jnp.sum(functools.reduce(jnp.add, weights), axis=1, keepdims=True)
        total = total[:heads] + total[heads:]
        acc = jnp.zeros((2 * heads, 2 * head_dim), F32)
        for c in range(half // 256):
            values = jnp.concatenate([vb[b, c * 256:(c + 1) * 256, :], vb[b, half + c * 256:half + (c + 1) * 256, :]], axis=1)
            p = jnp.concatenate([weights[2 * c], weights[2 * c + 1]], axis=1).astype(BF16)
            acc = acc + jnp.dot(p, values, preferred_element_type=F32)
        ctx = acc[:heads, :head_dim] + acc[heads:, head_dim:]
        csend[g, :, j:j + 1, :] = ctx.reshape(heads, 1, head_dim)
        stats = jnp.where(first_stat, top, total)
        csend[g, :, chunk + j:chunk + j + 1, :] = stats.reshape(heads, 1, LANES)

    def attend_of(g):
        for j in range(chunk):
            attend(g, j)
        for peer in peers:
            remote(csend.at[g, peer], crecv.at[g, me], ctx_ssem.at[0], ctx_rsem.at[0], {'sp': peer}).start()
        crecv[g, me] = csend[g, me]

    content_of(0)
    rel_out(2, lambda copy: copy.start())
    content_of(1)
    rel_out(3, lambda copy: copy.start())
    content_of(2)
    content_of(3)
    up_cols = half_ff // batch
    first_up = len(copies)
    up_groups = aall.shape[0] // CORES
    for t in range(batch):
        fetch(wu_hbm.at[:, pl.ds(pl.multiple_of(core * half_ff + t * up_cols, up_cols), up_cols)], kb.at[t],
              first_up + t // (batch // up_groups))
    for g in range(chunks):
        rel_in(g)
    for g in range(chunks):
        rel_done(g)
        v_copies[g].wait()
        attend_of(g)

    arrived(0, kvrecv)
    k_new, v_new = kvrecv[0, 0], kvrecv[0, 1]
    for p in range(1, n_sp):
        k_new, v_new = k_new + kvrecv[p, 0], v_new + kvrecv[p, 1]
    k_new = k_new.astype(BF16).astype(F32)
    v_new = v_new.astype(BF16).astype(F32)
    q_cont = (qall[me] + jnp.sum(jnp.where(lax.broadcasted_iota(jnp.int32, (heads, head_dim), 0) == me, u_wide, 0.0), axis=0, keepdims=True))
    q_cont = q_cont.astype(BF16).astype(F32)
    last_row = (n_sp - 1 - CORES * chip) * rel_rows + rel_rows - 1
    zero_dist = jnp.concatenate([part[:, pl.ds(last_row, 1), :].reshape(chunk, LANES) for part in grid_rel], axis=0)
    lane_b = lax.broadcasted_iota(jnp.int32, (batch, LANES), 1)
    rel0 = jnp.sum(jnp.where(lane_b == LANES - heads + me, zero_dist, 0.0), axis=1, keepdims=True)
    s_new = (jnp.sum(q_cont * k_new, axis=1, keepdims=True) + rel0) * scale

    later(csend.at[:, others], ctx_ssem.at[0])
    take(crecv.at[:, others], ctx_rsem.at[0])
    parts = [jnp.concatenate([crecv[g, p, :chunk] for g in range(chunks)], axis=0) for p in range(n_sp)]
    stats = [jnp.concatenate([crecv[g, p, chunk:] for g in range(chunks)], axis=0) for p in range(n_sp)]
    tops = [t[:, :1] for t in stats]
    sums = [t[:, LANES - 1:] for t in stats]
    best = functools.reduce(jnp.maximum, tops, s_new)
    e_new = jnp.exp(s_new - best)
    denom = e_new
    numer = e_new.astype(BF16).astype(F32) * v_new
    for p in range(n_sp):
        factor = jnp.exp(tops[p] - best)
        denom = denom + factor * sums[p]
        numer = numer + factor * parts[p]
    call[me] = (numer / denom).astype(BF16).astype(F32)
    gather(1, call)
    arrived(1, call)

    ctx_all = jnp.concatenate([call[h].astype(BF16) for h in range(heads)], axis=1)
    wo_copy.wait()
    parts_out, cp = aosend.shape[0], aosend.shape[2]
    attn_part = jnp.dot(ctx_all, wob[...], preferred_element_type=F32)
    for i in range(parts_out):
        aosend[i] = attn_part[:, i * cp:(i + 1) * cp]
        tp_send(0, i, aosend, aorecv)
    for i in range(parts_out):
        attn = tp_total(0, i, aorecv)
        x1_cols = pl.ds(pl.multiple_of(me * co + i * cp, cp), cp)
        x1all[me, i] = (hid[:, x1_cols].astype(F32) + attn).astype(BF16).astype(F32)
        gather(2, x1all, i)
    arrived(2, x1all)
    x1_parts = [x1all[p, i] for p in range(n_sp) for i in range(parts_out)]
    mean_sq = functools.reduce(jnp.add, [jnp.sum(t * t, axis=-1, keepdims=True) for t in x1_parts]) / (co * n_sp)
    inv = lax.rsqrt(mean_sq + EPS)
    gain = gm[...].reshape(1, co * n_sp).astype(F32)
    normed_mid = jnp.concatenate([(t * inv * gain[:, p * cp:(p + 1) * cp]).astype(BF16) for p, t in enumerate(x1_parts)], axis=1)
    per_part = aall.shape[2] // up_cols
    for i in range(aall.shape[0] // CORES):
        tiles_up = kb.at[i * per_part:(i + 1) * per_part]
        pltpu.make_async_copy(tiles_up, tiles_up, hsem.at[first_up + i]).wait()
        at = core * (aall.shape[0] // CORES) + i
        weights = jnp.concatenate([kb[t] for t in range(i * per_part, (i + 1) * per_part)], axis=1)
        up = jnp.dot(normed_mid, weights, preferred_element_type=F32)
        aall[at] = jax.nn.gelu(up, approximate=True).astype(BF16).astype(F32)
        remote(aall.at[at], aall.at[at], a_ssem.at[0], a_rsem.at[0], {'sp': sibling}).start()
    later(aall.at[0:up_groups], a_ssem.at[0])

    def down_of(which):
        act = jnp.concatenate([aall[which * up_groups + i].astype(BF16) for i in range(up_groups)], axis=1)
        units = pl.ds(pl.multiple_of(which * half_ff, half_ff), half_ff)
        return jnp.dot(act, wdb[units, :], preferred_element_type=F32)

    wd_copy.wait()
    down_part = down_of(core)
    take(aall.at[0:up_groups], a_rsem.at[0])
    down_part = down_part + down_of(1 - core)
    for i in range(parts_out):
        dnsend[i] = down_part[:, i * cp:(i + 1) * cp]
        tp_send(1, i, dnsend, dnrecv)
    for i in range(parts_out):
        down = tp_total(1, i, dnrecv)
        oall[me, i] = (x1all[me, i] + down).astype(BF16).astype(F32)
        gather(3, oall, i)
    arrived(3, oall)
    for p in range(n_sp):
        for i in range(parts_out):
            out_ref[:, p * co + i * cp:p * co + (i + 1) * cp] = oall[p, i].astype(BF16)
    for wait in sends:
        wait()
    rel_sent()


def solution(mesh):
    n_sp, n_tp = mesh.shape['sp'], mesh.shape['tp']
    spec_rows = P('dp', None)
    spec_cache = P('dp', 'sp', 'tp', None)
    in_specs = (spec_rows, spec_cache, spec_cache, P('dp'), P('sp', 'tp', None), P('tp', None), P('tp', None), P(None), P(None, 'tp', None), P(None, 'tp', None), P(None, 'tp', None), P('tp', None, None), P(None), P(None, 'tp'), P('tp', None))
    out_specs = spec_rows

    def layer_step(hidden, k_cache, v_cache, lengths, rel_table, u_bias, w_bias, g_attn, w_query, w_key, w_value, w_out, g_mlp, w_up, w_down):
        batch, seq_blk, heads, head_dim = k_cache.shape
        width = hidden.shape[1]
        ff = w_up.shape[1]
        rows = seq_blk * heads
        kk = width // n_sp
        co = width // n_sp
        rel_rows = rows // LANES
        vmem = functools.partial(pl.BlockSpec, memory_space=pltpu.VMEM)
        hbm = functools.partial(pl.BlockSpec, memory_space=pl.ANY)
        dma = pltpu.SemaphoreType.DMA
        phases = 4
        return pl.pallas_call(
            functools.partial(layer_kernel, n_sp, n_tp),
            out_shape=jax.ShapeDtypeStruct((batch, width), BF16),
            in_specs=[hbm()] * 15,
            out_specs=vmem(),
            scratch_shapes=[
                pltpu.SMEM((batch,), jnp.int32),
                pltpu.VMEM((batch, width), BF16),
                pltpu.VMEM((heads, head_dim), BF16),
                pltpu.VMEM((heads, head_dim), BF16),
                pltpu.VMEM((width,), BF16),
                pltpu.VMEM((width,), BF16),
                pltpu.VMEM((width * heads, head_dim), BF16),
                pltpu.VMEM((2, kk * heads, head_dim), BF16),
                pltpu.VMEM((width // LANES * batch, LANES), BF16),
                pltpu.VMEM((width // LANES * batch, LANES * heads), BF16),
                pltpu.VMEM((seq_blk, heads, head_dim), BF16),
                pltpu.VMEM((rows, head_dim), BF16),
                pltpu.VMEM((batch, rows, head_dim), BF16),
                pltpu.VMEM((batch, rows, head_dim), BF16),
                pltpu.VMEM((heads * head_dim, co), BF16),
                pltpu.VMEM((ff, co), BF16),
                pltpu.VMEM((n_sp, 2, batch, head_dim), F32),
                pltpu.VMEM((n_sp, 2, batch, head_dim), F32),
                pltpu.VMEM((n_sp, batch, head_dim), F32),
                pltpu.VMEM((batch, heads, head_dim), F32),
                pltpu.VMEM((batch, rel_rows, LANES), F32),
                *[pltpu.VMEM((batch // CHUNKS, (n_sp + 1) * rel_rows + 8, LANES), F32)] * CHUNKS,
                pltpu.VMEM((batch, rel_rows, LANES), F32),
                pltpu.VMEM((batch, 2 * heads, rows // 2), F32),
                pltpu.VMEM((CHUNKS, n_sp, 2 * batch // CHUNKS, head_dim), F32),
                pltpu.VMEM((CHUNKS, n_sp, 2 * batch // CHUNKS, head_dim), F32),
                pltpu.VMEM((n_sp, batch, head_dim), F32),
                pltpu.VMEM((OUT_PARTS, batch, co // OUT_PARTS), F32),
                pltpu.VMEM((OUT_PARTS, n_tp, batch, co // OUT_PARTS), F32),
                pltpu.VMEM((n_sp, OUT_PARTS, batch, co // OUT_PARTS), F32),
                pltpu.VMEM((UP_PARTS, batch, ff // UP_PARTS), F32),
                pltpu.VMEM((OUT_PARTS, batch, co // OUT_PARTS), F32),
                pltpu.VMEM((OUT_PARTS, n_tp, batch, co // OUT_PARTS), F32),
                pltpu.VMEM((n_sp, OUT_PARTS, batch, co // OUT_PARTS), F32),
                dma((19 + 3 * CHUNKS + UP_PARTS // CORES,)),
                dma((phases,)),
                dma((phases,)),
                dma((n_sp // CORES,)),
                dma((n_sp // CORES, CHUNKS)),
                dma((n_sp // CORES,)),
                dma((n_sp // CORES, CHUNKS)),
                dma((1,)),
                dma((1,)),
                dma((CHUNKS,)),
                dma((1,)),
                dma((1,)),
                dma((1,)),
                dma((1,)),
                dma((2, OUT_PARTS)),
                dma((2, OUT_PARTS)),
            ],
            compiler_params=pltpu.CompilerParams(collective_id=0, has_side_effects=True, vmem_limit_bytes=67043328),
            name='decode_layer',
        )(lengths, hidden, u_bias, w_bias, g_attn, g_mlp, rel_table,
          k_cache.reshape(batch, rows, head_dim), v_cache.reshape(batch, rows, head_dim),
          w_query.reshape(width * heads, head_dim), w_key.reshape(width * heads, head_dim), w_value.reshape(width * heads, head_dim),
          w_out.reshape(heads * head_dim, width), w_up, w_down)

    return jax.shard_map(layer_step, mesh=mesh, in_specs=in_specs, out_specs=out_specs, check_vma=False)
```

profile of v0, /device:TPU:97, one launch (start us, length us, event | category | flops | bytes accessed | tf_op | source)
XLA Modules:
  0.0 58.1 jit_solution(1210377353233460062)
XLA Ops:
  0.0 56.6 %decode_layer.1 = bf16[16,4096]{1,0:T(8,128)(2,1)} custom-call(s32[16]{0:T(128)} %lens_in.1, bf16[16,4096]{1,0:T(8,128)(2,1)} %hid_in.1, bf16[8,128]{1,0:T(8,128)(2,1)} %u_in.1, bf16[8,128]{1,0:T(8,128)(2,1)} %w_in.1, bf16[4096]{0:T(1024)(128)(2,1)} %ga_in.1, bf16[4096]{0:T(1024)(128)(2,1)} %gm_in.1, bf16[512,8,128]{2,1,0:T(8,128)(2,1)} %rel_hbm.1, ...), custom_call_target="tpu_custom_call" | custom-call | tf_op jit(solution)/shard_map/decode_layer/pallas_call | solution.py:492
  56.6 1.6 %copy.17 = bf16[16,4096]{1,0:T(8,128)(2,1)} copy(bf16[16,4096]{1,0:T(8,128)(2,1)} %decode_layer.1) | data formatting | bytes 262144
where the time goes:
time: 58.2 us; the launch traced here: 58.1 us
  Pallas kernels  56.6 us (97%)
  local copies, waits for them, and re-layouts  1.57 us (3%)
    pallas_call x1, Pallas kernels, layer_step(): pl.pallas_call(functools.partial(layer_kernel, n_sp, n_tp), out_shape=jax...  56.6 us
    unnamed x1, local copies, waits for them, and re-layouts  1.57 us

commit v1 on v0

--- a/solution.py
+++ b/solution.py
@@ -207,22 +207,28 @@
     def needed(a, b):
         return a + b <= chips - 1
 
-    def rel_out(g, act):
-        for dx in range(1, chips):
-            to_chip = lax.rem(chip + dx, chips)
-
-            @pl.when(needed(to_chip, chip))
-            def _():
-                for part in range(CORES):
-                    if 2 * dx == chips and part == 1:
-                        continue
-                    act(remote(relsend.at[seqs(g), part * half_rows:(part + 1) * half_rows, :],
-                               spot(me, to_chip, g, part * half_rows, half_rows),
-                               rel_ssem.at[dx], rel_rsem.at[chip, g], {'sp': to_chip * CORES + part}))
+    def rel_out(dx, parts):
+        to_chip = lax.rem(chip + dx, chips)
+
+        @pl.when(needed(to_chip, chip))
+        def _():
+            for g in range(chunks):
+                for part in parts:
+                    remote(relsend.at[seqs(g), part * half_rows:(part + 1) * half_rows, :],
+                           spot(me, to_chip, g, part * half_rows, half_rows),
+                           rel_ssem.at[dx], rel_rsem.at[chip, g], {'sp': to_chip * CORES + part}).start()
+
+    def rel_out_first():
+        rel_out(chips - 1, (1,))
+        rel_out(chips // 2, (0,))
+        for dx in range(1, chips - 1):
+            if 2 * dx != chips:
+                rel_out(dx, (0, 1))
 
         @pl.when(needed(chip, chip))
         def _():
-            act(remote(relsend.at[seqs(g)], spot(me, chip, g, 0, rel_rows), sib_ssem.at[0], sib_rsem.at[g], {'sp': sibling}))
+            for g in range(chunks):
+                remote(relsend.at[seqs(g)], spot(me, chip, g, 0, rel_rows), sib_ssem.at[0], sib_rsem.at[g], {'sp': sibling}).start()
 
     def each_source(fn):
         for dx in range(1, chips):
@@ -246,13 +252,28 @@
 
     both = relsend.at[0:chunk]
 
-    def rel_in(g):
-        def fn(dx, from_chip):
+    def source_in(g, dx):
+        from_chip = lax.rem(chip + dx, chips)
+
+        @pl.when(needed(from_chip, chip))
+        def _():
             take(both, rel_rsem.at[from_chip, g])
             for c in range(CORES):
                 pass_on(g, dx, from_chip, c, lambda copy: copy.start())
 
-        each_source(fn)
+    def rel_in_first():
+        @pl.when(core == 1)
+        def _():
+            for g in range(chunks):
+                source_in(g, 1)
+
+    def rel_in(g):
+        @pl.when(core == 0)
+        def _():
+            source_in(g, 1)
+
+        for dx in range(2, chips):
+            source_in(g, dx)
 
     def rel_done(g):
         each_source(lambda dx, from_chip: take(both, fwd_rsem.at[from_chip, g]))
@@ -282,7 +303,7 @@
             remote(relsend, relsend, relay_ssem.at[0], relay_ssem.at[0], {'sp': sibling}).wait_send()
 
     pl.semaphore_wait(barrier, n_sp + n_tp - 2)
-    rel_out(0, lambda copy: copy.start())
+    rel_out_first()
 
     @pl.when(needed(chip, chip))
     def _():
@@ -303,7 +324,6 @@
     scatter(0, kvsend, kvrecv)
     kvrecv[me] = kvsend[me]
 
-    rel_out(1, lambda copy: copy.start())
     for h in range(heads):
         qcb[:, h:h + 1, :] = (qall[h] + u_wide[h:h + 1]).reshape(batch, 1, head_dim)
 
@@ -366,10 +386,10 @@
         crecv[g, me] = csend[g, me]
 
     content_of(0)
-    rel_out(2, lambda copy: copy.start())
+    rel_out(chips - 1, (0,))
     content_of(1)
-    rel_out(3, lambda copy: copy.start())
     content_of(2)
+    rel_in_first()
     content_of(3)
     up_cols = half_ff // batch
     first_up = len(copies)
@@ -377,9 +397,11 @@
     for t in range(batch):
         fetch(wu_hbm.at[:, pl.ds(pl.multiple_of(core * half_ff + t * up_cols, up_cols), up_cols)], kb.at[t],
               first_up + t // (batch // up_groups))
+    rel_in(0)
+    rel_in(1)
     for g in range(chunks):
-        rel_in(g)
-    for g in range(chunks):
+        if 0 < g < chunks - 1:
+            rel_in(g + 1)
         rel_done(g)
         v_copies[g].wait()
         attend_of(g)

time: 58.2 us -> 56.1 us (0.964)
  Pallas kernels: 56.6 us -> 54.5 us
    pallas_call x1, Pallas kernels: 56.6 us -> 54.5 us  [layer_step(): pl.pallas_call(functools.partial(layer_kernel, n_sp, n_tp), out_shape=jax...]
where the time goes in v1:
time: 56.1 us; the launch traced here: 56 us
  Pallas kernels  54.5 us (97%)
  local copies, waits for them, and re-layouts  1.57 us (3%)
    pallas_call x1, Pallas kernels, layer_step(): pl.pallas_call(functools.partial(layer_kernel, n_sp, n_tp), out_shape=jax...  54.5 us
    unnamed x1, local copies, waits for them, and re-layouts  1.57 us

profile of v1, /device:TPU:97, one launch (start us, length us, event | category | flops | bytes accessed | tf_op | source)
XLA Modules:
  0.0 56.0 jit_solution(8396434315816833003)
XLA Ops:
  0.0 54.5 %decode_layer.1 = bf16[16,4096]{1,0:T(8,128)(2,1)} custom-call(s32[16]{0:T(128)} %lens_in.1, bf16[16,4096]{1,0:T(8,128)(2,1)} %hid_in.1, bf16[8,128]{1,0:T(8,128)(2,1)} %u_in.1, bf16[8,128]{1,0:T(8,128)(2,1)} %w_in.1, bf16[4096]{0:T(1024)(128)(2,1)} %ga_in.1, bf16[4096]{0:T(1024)(128)(2,1)} %gm_in.1, bf16[512,8,128]{2,1,0:T(8,128)(2,1)} %rel_hbm.1, ...), custom_call_target="tpu_custom_call" | custom-call | tf_op jit(solution)/shard_map/decode_layer/pallas_call | solution.py:514
  54.5 1.6 %copy.17 = bf16[16,4096]{1,0:T(8,128)(2,1)} copy(bf16[16,4096]{1,0:T(8,128)(2,1)} %decode_layer.1) | data formatting | bytes 262144
